TPU v7x, 32 devices: a whole 2x2x4 slice. The times are simulated.
32 devices in a mesh: shock: 2 (over core), ty: 4 (over y, x), tz: 4 (over z).
Axes of the slice: x: 2, y: 2, z: 4, core: 2. Of those that a mesh axis runs over, the one named last changes fastest.
Arguments:
- jitter: float32 [3, 8, 4, 32, 512], P(None, None, 'shock', 'ty', 'tz'), may hold values from -0.1 to 0.1
- counts: int32 [4, 32, 512], P('shock', 'ty', 'tz'), may hold values from 2 to 8
- inflow_jitter: float32 [3, 8, 32, 512], P(None, None, 'ty', 'tz'), may hold values from -0.1 to 0.1
- inflow_counts: int32 [32, 512], P('ty', 'tz'), may hold values from 2 to 8
- embed_weights: float32 [16], replicated, may hold values from -1.2 to 1.2
Outputs:
- forces: float32 [3, 8, 4, 32, 512], P(None, None, 'shock', 'ty', 'tz')
- energy: float32 [8, 4, 32, 512], P(None, 'shock', 'ty', 'tz')
Inputs may be any that keep to these rules, and one draw needn't show every extreme that they name: `counts`: occupied slots per cell, of 8. `inflow_counts`: occupied slots per entering cell, of 8.
All inputs are finite; a program needn't handle non-finite values.
Results may differ from a plain program's by a relative error of at most 0.0003.
Values sent between devices are 32-bit elements; how exact they have to be, the bound alone decides.
A program may use at most 64 MiB of HBM per device.

v0:
```python
import functools

import jax
import jax.numpy as jnp
from jax import lax
from jax.experimental import pallas as pl
from jax.experimental.pallas import tpu as pltpu
from jax.sharding import PartitionSpec as P

MESH = pl.DeviceIdType.MESH
FAR = 8.0
ALL = [
    (x, y, z)
    for x in range(-2, 3)
    for y in range(-2, 3)
    for z in range(-2, 3)
    if (x, y, z) != (0, 0, 0) and (abs(x) == 2) + (abs(y) == 2) + (abs(z) == 2) <= 1
]
PARTS = [[o for o in ALL if (o[1] in (0, 1), o[2] in (0, 1)) == inside]
         for inside in ((True, True), (False, True), (True, False), (False, False))]
OFFSETS = sum(PARTS, [])
STARTS = [sum(len(p) for p in PARTS[:k]) for k in range(len(PARTS))]
DIRS = [(b, c) for b in (-1, 0, 1) for c in (-1, 0, 1) if (b, c) != (0, 0)]
ROW_DIRS = (1, 6)
COL_DIRS = (3, 4)
CORNER_DIRS = (0, 2, 5, 7)
ORDER = CORNER_DIRS + COL_DIRS + ROW_DIRS
SLOTS = 8
RIM = 2
LOG2E = 1.4426950408889634


def side(step):
    return 0 if step < 0 else 1


def kernel(sizes, jit_hbm, cnt_hbm, ijit_hbm, icnt_hbm, weights_hbm, forces, energy,
           jit, cnt, ijit, icnt, weights, dens, load, atoms, rows_out, cols_out, corn_out, rows_in, cols_in, corn_in,
           site, terms, slope, emb, slope_site,
           srow_out, scol_out, srow_in, scol_in, scor_in, slayer_in,
           send1, recv1, send_layer, recv_layer, send2, recv2, send_s, recv_s):
    n_shock, n_ty, n_tz = sizes
    layers, ny, nz = cnt.shape
    ext = layers + RIM
    me, my, mz = (lax.axis_index(a) for a in ("shock", "ty", "tz"))
    leading = me == 0
    trailing = me == n_shock - 1
    lane = lax.broadcasted_iota(jnp.int32, (ny, nz), 1)
    row = lax.broadcasted_iota(jnp.int32, (ny, nz), 0)

    def device(a, b, c):
        return (me + a, lax.rem(my + b + n_ty, n_ty), lax.rem(mz + c + n_tz, n_tz))

    def exists(a):
        return None if a == 0 else (me > 0 if a < 0 else me < n_shock - 1)

    def guarded(a, fn):
        cond = exists(a)
        if cond is None:
            fn()
        else:
            pl.when(cond)(fn)

    loads = [pltpu.make_async_copy(src, dst, load.at[k]) for k, (src, dst) in enumerate(
        ((cnt_hbm, cnt), (jit_hbm, jit), (icnt_hbm, icnt), (ijit_hbm, ijit), (weights_hbm, weights)))]
    for copy in loads:
        copy.start()

    barrier = pltpu.get_barrier_semaphore()
    for a in (-1, 0, 1):
        def greet(a=a):
            for b in (-1, 0, 1):
                for c in (-1, 0, 1):
                    if (a, b, c) != (0, 0, 0):
                        pl.semaphore_signal(barrier, inc=1, device_id=device(a, b, c), device_id_type=MESH)
        guarded(a, greet)

    def atom_rows(layer, c, s):
        return pl.ds(((layer * 3 + c) * SLOTS + s) * ny, ny)

    for copy in loads:
        copy.wait()
    for l in range(layers):
        count = cnt[l]
        if l == 0:
            count = jnp.where(leading, 0, count)
        for s in range(SLOTS):
            for c in range(3):
                value = jit[c, s, l] + (0.25 + 0.5 * (s // 2**c % 2))
                if c == 0:
                    value = jnp.where(s < count, value, value + FAR)
                atoms[atom_rows(l, c, s), :] = value

    def place(value, source, target):
        shift = (target - source) % nz
        return value if shift == 0 else pltpu.roll(value, shift, 1)

    def pack(g, base):
        for l in range(RIM):
            for yi, edge in ((0, 0), (1, ny - 1)):
                found = []
                for c in range(3):
                    start = ((base + l) * 3 + c) * SLOTS * ny + edge
                    value = atoms[pl.ds(start, SLOTS, stride=ny), :]
                    rows_out[g, yi, l, c] = value
                    found.append(value)
                for zi, zedge in ((0, 0), (1, nz - 1)):
                    packed = place(found[0], zedge, 0)
                    for c in (1, 2):
                        packed = jnp.where(lane == c, place(found[c], zedge, c), packed)
                    corn_out[g, yi, zi, l] = packed
            for zi, zedge in ((0, 0), (1, nz - 1)):
                parts = []
                for c in range(3):
                    packed = None
                    for s in range(SLOTS):
                        k = c * SLOTS + s
                        moved = place(atoms[atom_rows(base + l, c, s), :], zedge, k)
                        packed = moved if packed is None else jnp.where(lane == k, moved, packed)
                    parts.append(packed)
                packed = jnp.where(lane < SLOTS, parts[0], jnp.where(lane < 2 * SLOTS, parts[1], parts[2]))
                cols_out[g, zi, l] = packed

    pack(0, 0)

    @pl.when(trailing)
    def _():
        count = icnt[...]
        for s in range(SLOTS):
            for c in range(3):
                base = 0.25 + 0.5 * (s // 2**c % 2)
                value = ijit[c, s] + base
                if c == 0:
                    value = jnp.where(s < count, value, value + FAR)
                atoms[atom_rows(layers, c, s), :] = value
                atoms[atom_rows(layers + 1, c, s), :] = jnp.full((ny, nz), base + (FAR if c == 0 else 0.0), jnp.float32)
        pack(1, layers)

    ends = jnp.where(leading, 1, 0) + jnp.where(trailing, 1, 0)
    pl.semaphore_wait(barrier, 26 - 9 * ends)

    layer_rows = 3 * SLOTS * ny

    def layer_copy():
        return pltpu.make_async_remote_copy(
            src_ref=atoms.at[pl.ds(0, RIM * layer_rows)],
            dst_ref=atoms.at[pl.ds(layers * layer_rows, RIM * layer_rows)],
            send_sem=send_layer, recv_sem=recv_layer,
            device_id=device(-1, 0, 0), device_id_type=MESH)

    def ends1(g, h, b, c):
        if c == 0:
            return rows_out.at[g, side(b)], rows_in.at[h, side(-b)]
        if b == 0:
            return cols_out.at[g, side(c)], cols_in.at[h, side(-c)]
        return corn_out.at[g, side(b), side(c)], corn_in.at[h, side(-b), side(-c)]

    def copy1(group, g, h, a, d):
        b, c = DIRS[d]
        src, dst = ends1(g, h, b, c)
        return pltpu.make_async_remote_copy(
            src_ref=src, dst_ref=dst, send_sem=send1.at[group, d],
            recv_sem=recv1.at[h, len(DIRS) - 1 - d],
            device_id=device(a, b, c), device_id_type=MESH)

    groups = ((0, 0, 0, 0, None), (1, 0, 1, -1, me > 0), (2, 1, 1, 0, trailing))

    def for_groups(fn):
        for group, g, h, a, cond in groups:
            def run(group=group, g=g, h=h, a=a):
                for d in ORDER:
                    fn(copy1(group, g, h, a, d))
            if cond is None:
                run()
            else:
                pl.when(cond)(run)

    pl.when(me > 0)(lambda: layer_copy().start())
    for_groups(lambda copy: copy.start())

    pl.when(me < n_shock - 1)(lambda: layer_copy().wait_recv())
    def arrived(dirs):
        for h in range(2):
            for d in dirs:
                copy1(0, 0, h, 0, d).wait_recv()

    def with_edge_z(value, column, source, step):
        edge = nz - 1 if step > 0 else 0
        return jnp.where(lane == edge, place(column, source, edge), pltpu.roll(value, (-step) % nz, 1))

    def with_edge_y(value, halo, s, step):
        edge = ny - 1 if step > 0 else 0
        return jnp.where(row == edge, jnp.broadcast_to(halo[s:s + 1, :], (ny, nz)),
                         pltpu.roll(value, (-step) % ny, 0))

    def sites_of(e, c, s, b, z):
        bx, by, bz = s % 2, s // 2 % 2, s // 4 % 2
        return c, 2 * e + bx, 2 * (b + 1) + by, 2 * (z + 1) + bz

    def moved(value, c, b, z):
        return value + float(b) if c == 1 and b else (value + float(z) if c == 2 and z else value)

    def build_centre(e, carry):
        x_base = e.astype(jnp.float32)
        for c in range(3):
            for s in range(SLOTS):
                value = atoms[pl.ds(pl.multiple_of(((e * 3 + c) * SLOTS + s) * ny, ny), ny), :]
                site[sites_of(e, c, s, 0, 0)] = value + x_base if c == 0 else value
        return carry

    def halo_rows(e, c, b):
        halo = rows_in[e // RIM, side(b), e % RIM, c]
        return halo + e.astype(jnp.float32) if c == 0 else halo

    def build_y(e, carry):
        for c in range(3):
            for b in (-1, 1):
                halo = halo_rows(e, c, b)
                for s in range(SLOTS):
                    out = with_edge_y(site[sites_of(e, c, s, 0, 0)], halo, s, b)
                    site[sites_of(e, c, s, b, 0)] = moved(out, c, b, 0)
        return carry

    def build_z(e, carry):
        for z in (-1, 1):
            columns = cols_in[e // RIM, side(z), e % RIM]
            first = columns + e.astype(jnp.float32)
            for c in range(3):
                for s in range(SLOTS):
                    out = with_edge_z(site[sites_of(e, c, s, 0, 0)], columns if c else first, c * SLOTS + s, z)
                    site[sites_of(e, c, s, 0, z)] = moved(out, c, 0, z)
        return carry

    def build_corners(e, carry):
        for c in range(3):
            for b in (-1, 1):
                halo = halo_rows(e, c, b)
                for z in (-1, 1):
                    corner = corn_in[e // RIM, side(b), side(z), e % RIM]
                    if c == 0:
                        corner = corner + e.astype(jnp.float32)
                    halo_z = moved(with_edge_z(halo, corner, c, z), c, 0, z)
                    for s in range(SLOTS):
                        out = with_edge_y(site[sites_of(e, c, s, 0, z)], halo_z, s, b)
                        site[sites_of(e, c, s, b, z)] = out + float(b) if c == 1 else out
        return carry

    def split(q):
        return 2 + q // 4, 2 + q // 2 % 2, 2 + q % 2

    def place_of(q):
        x, y, z = split(q)
        return x // 2 - 1, x % 2 + 2 * (y - 2) + 4 * (z - 2)

    def near(q, offset):
        x, y, z = split(q)
        return (x + offset[0], y + offset[1] * (5 - 2 * y), z + offset[2] * (5 - 2 * z))

    atoms_count = 2 * layers * 4

    def density_part(part, q, carry):
        at = split(q)
        px, py, pz = (site[(c,) + at] for c in range(3))
        zero = jnp.zeros((ny, nz), jnp.float32)
        total = [dens[q] if part else zero, zero]
        for k, offset in enumerate(PARTS[part]):
            n = STARTS[part] + k
            to = near(q, offset)
            dx = site[(0,) + to] - px
            dy = site[(1,) + to] - py
            dz = site[(2,) + to] - pz
            squared = dx * dx + dy * dy + dz * dz
            inverse = lax.rsqrt(squared)
            radius = squared * inverse
            inside = jnp.maximum(1.0 - radius, 0.0)
            decay = jnp.exp(1.5 - 3.0 * radius)
            inside2 = inside * inside
            total[k % 2] = total[k % 2] + decay * (inside2 * inside2)
            terms[0, q, n] = inside
            terms[1, q, n] = decay
            terms[2, q, n] = inverse
        if part < len(PARTS) - 1:
            dens[q] = total[0] + total[1]
            return carry
        l, s = place_of(q)
        density = (total[0] + total[1]) * (16.0 / 6.0)
        root = jnp.sqrt(1.0 + density)
        value = -root
        grad = -0.5 / root
        for k in range(weights.shape[0]):
            scaled = density * 4.0 - float(k)
            bump = weights[k] * jnp.exp(-0.5 * scaled * scaled)
            value = value + bump
            grad = grad - bump * scaled * 4.0
        emb[q] = value
        slope[pl.ds(pl.multiple_of((l * SLOTS + s) * ny, ny), ny), :] = grad
        return carry

    for part, (dirs, build) in enumerate((
            ((), build_centre), (ROW_DIRS, build_y), (COL_DIRS, build_z), (CORNER_DIRS, build_corners))):
        arrived(dirs)
        lax.fori_loop(0, ext, build, 0)
        lax.fori_loop(0, atoms_count, functools.partial(density_part, part), 0)

    for l in range(layers):
        for yi, edge in ((0, 0), (1, ny - 1)):
            srow_out[yi, l] = slope[pl.ds(l * SLOTS * ny + edge, SLOTS, stride=ny), :]
        for zi, zedge in ((0, 0), (1, nz - 1)):
            packed = None
            for s in range(SLOTS):
                moved = place(slope[pl.ds((l * SLOTS + s) * ny, ny), :], zedge, s)
                packed = moved if packed is None else jnp.where(lane == s, moved, packed)
            scol_out[zi, l] = packed

    def ends2(a, b, c):
        if c == 0:
            return srow_out.at[side(b)], srow_in.at[1 - a, side(-b)]
        if b == 0:
            return scol_out.at[side(c)], scol_in.at[1 - a, side(-c)]
        return srow_out.at[side(b)], scor_in.at[1 - a, side(-b), side(-c)]

    def copy2(a, d):
        b, c = DIRS[d]
        src, dst = ends2(a, b, c)
        return pltpu.make_async_remote_copy(
            src_ref=src, dst_ref=dst, send_sem=send2.at[a + 1, d],
            recv_sem=recv2.at[1 - a, len(DIRS) - 1 - d],
            device_id=device(a, b, c), device_id_type=MESH)

    def slope_copy(a):
        first = 0 if a < 0 else layers - 1
        return pltpu.make_async_remote_copy(
            src_ref=slope.at[pl.ds(first * SLOTS * ny, SLOTS * ny)], dst_ref=slayer_in.at[side(-a)],
            send_sem=send_s.at[side(a)], recv_sem=recv_s.at[side(-a)],
            device_id=device(a, 0, 0), device_id_type=MESH)

    for a in (-1, 1, 0):
        def run(a=a):
            if a:
                slope_copy(a).start()
            for d in ORDER:
                copy2(a, d).start()
        guarded(a, run)

    def pair_step(q, carry):
        pair = [jnp.zeros((ny, nz), jnp.float32) for _ in range(2)]
        for n in range(len(OFFSETS)):
            inside, decay, inverse = (terms[i, q, n] for i in range(3))
            cube = inside * inside * inside * decay
            lower = decay - 2.0
            pair[n % 2] = pair[n % 2] + cube * inside * lower
            scaled = cube * inverse
            terms[0, q, n] = scaled * (-8.0 * inside - 32.0 / 3.0)
            terms[1, q, n] = scaled * (-19.2 * inside * (decay - 1.0) - 12.8 * lower)
        emb[q] = emb[q] + (0.5 * 3.2) * (pair[0] + pair[1])
        return carry

    lax.fori_loop(0, atoms_count, pair_step, 0)

    for a in (-1, 1):
        @pl.when(jnp.logical_not(exists(a)))
        def _(a=a):
            slayer_in[side(a)] = jnp.zeros(slayer_in.shape[1:], jnp.float32)
            srow_in[a + 1] = jnp.zeros(srow_in.shape[1:], jnp.float32)
            scol_in[a + 1] = jnp.zeros(scol_in.shape[1:], jnp.float32)
            scor_in[a + 1] = jnp.zeros(scor_in.shape[1:], jnp.float32)

    def slope_at(e, s, b, z):
        return sites_of(e, 0, s, b, z)[1:]

    def slopes_arrived(dirs):
        for a in (-1, 0, 1):
            def run(a=a):
                if a and not dirs:
                    slope_copy(-a).wait_recv()
                for d in dirs:
                    copy2(-a, d).wait_recv()
            guarded(a, run)

    def force_part(part, q, carry):
        x, y, z = split(q)
        l, s = place_of(q)
        at = (x, y, z)
        centre = [site[(c,) + at] for c in range(3)]
        own = slope_site[at]
        zero = jnp.zeros((ny, nz), jnp.float32)
        total = [[forces[c, s, l] if part else zero, zero] for c in range(3)]
        for k, offset in enumerate(PARTS[part]):
            n = STARTS[part] + k
            to = near(q, offset)
            weight = (own + slope_site[to]) * terms[0, q, n] + terms[1, q, n]
            for c in range(3):
                total[c][k % 2] = total[c][k % 2] + weight * (site[(c,) + to] - centre[c])
        if part < len(PARTS) - 1:
            for c in range(3):
                forces[c, s, l] = total[c][0] + total[c][1]
            return carry
        occupied = centre[0] - (x // 2).astype(jnp.float32) < 0.5 * FAR
        for c in range(3):
            forces[c, s, l] = jnp.where(occupied, total[c][0] + total[c][1], 0.0)
        energy[s, l] = jnp.where(occupied, emb[q], 0.0)
        return carry

    for part, dirs in enumerate(((), ROW_DIRS, COL_DIRS, CORNER_DIRS)):
        slopes_arrived(dirs)
        for e in range(layers + 2):
            a = 0 if e == 0 else (2 if e == layers + 1 else 1)
            l = layers - 1 if e == 0 else (0 if e == layers + 1 else e - 1)
            steps = (-1, 1)
            if part == 0:
                for s in range(SLOTS):
                    slope_site[slope_at(e, s, 0, 0)] = (
                        slope[pl.ds((l * SLOTS + s) * ny, ny), :] if a == 1
                        else slayer_in[a // 2, pl.ds(s * ny, ny), :])
            elif part == 1:
                for b in steps:
                    halo = srow_in[a, side(b), l]
                    for s in range(SLOTS):
                        slope_site[slope_at(e, s, b, 0)] = with_edge_y(
                            slope_site[slope_at(e, s, 0, 0)], halo, s, b)
            elif part == 2:
                for z in steps:
                    columns = scol_in[a, side(z), l]
                    for s in range(SLOTS):
                        slope_site[slope_at(e, s, 0, z)] = with_edge_z(
                            slope_site[slope_at(e, s, 0, 0)], columns, s, z)
            else:
                for b in steps:
                    for z in steps:
                        halo = with_edge_z(srow_in[a, side(b), l], scor_in[a, side(b), side(z), l],
                                           0 if z > 0 else nz - 1, z)
                        for s in range(SLOTS):
                            slope_site[slope_at(e, s, b, z)] = with_edge_y(
                                slope_site[slope_at(e, s, 0, z)], halo, s, b)
        lax.fori_loop(0, atoms_count, functools.partial(force_part, part), 0)

    pl.when(me > 0)(lambda: layer_copy().wait_send())
    for_groups(lambda copy: copy.wait_send())
    for a in (-1, 0, 1):
        def run(a=a):
            if a:
                slope_copy(a).wait_send()
            for d in range(len(DIRS)):
                copy2(a, d).wait_send()
        guarded(a, run)


def on_device(sizes, jitter, counts, inflow_jitter, inflow_counts, embed_weights):
    dims, slots, layers, ny, nz = jitter.shape
    assert slots == SLOTS and layers == RIM
    ext = layers + RIM
    f32 = jnp.float32
    tile = (ny, nz)
    vmem = pl.BlockSpec(memory_space=pltpu.VMEM)
    n = len(OFFSETS)
    dma = pltpu.SemaphoreType.DMA
    hbm = pl.BlockSpec(memory_space=pltpu.HBM)
    scratch = [
        pltpu.VMEM(jitter.shape, f32),
        pltpu.VMEM(counts.shape, counts.dtype),
        pltpu.VMEM(inflow_jitter.shape, f32),
        pltpu.VMEM(inflow_counts.shape, counts.dtype),
        pltpu.SMEM(embed_weights.shape, f32),
        pltpu.VMEM((layers * slots,) + tile, f32),
        dma((5,)),
        pltpu.VMEM((ext * dims * slots * ny, nz), f32),
        pltpu.VMEM((2, 2, RIM, dims) + (slots, nz), f32),
        pltpu.VMEM((2, 2, RIM) + tile, f32),
        pltpu.VMEM((2, 2, 2, RIM) + (slots, nz), f32),
        pltpu.VMEM((2, 2, RIM, dims) + (slots, nz), f32),
        pltpu.VMEM((2, 2, RIM) + tile, f32),
        pltpu.VMEM((2, 2, 2, RIM) + (slots, nz), f32),
        pltpu.VMEM((dims, 2 * ext, 6, 6) + tile, f32),
        pltpu.VMEM((3, layers * slots, n) + tile, f32),
        pltpu.VMEM((layers * slots * ny, nz), f32),
        pltpu.VMEM((layers * slots,) + tile, f32),
        pltpu.VMEM((2 * ext, 6, 6) + tile, f32),
        pltpu.VMEM((2, layers) + (slots, nz), f32),
        pltpu.VMEM((2, layers) + tile, f32),
        pltpu.VMEM((3, 2, layers) + (slots, nz), f32),
        pltpu.VMEM((3, 2, layers) + tile, f32),
        pltpu.VMEM((3, 2, 2, layers) + (slots, nz), f32),
        pltpu.VMEM((2, slots * ny, nz), f32),
        dma((3, len(DIRS))),
        dma((2, len(DIRS))),
        dma,
        dma,
        dma((3, len(DIRS))),
        dma((3, len(DIRS))),
        dma((2,)),
        dma((2,)),
    ]
    raw = pl.pallas_call(
        functools.partial(kernel, sizes),
        out_shape=(
            jax.ShapeDtypeStruct(jitter.shape, f32),
            jax.ShapeDtypeStruct(jitter.shape[1:], f32),
        ),
        in_specs=[hbm] * 5,
        out_specs=(vmem, vmem),
        scratch_shapes=scratch,
        compiler_params=pltpu.CompilerParams(
            collective_id=0, has_side_effects=True, vmem_limit_bytes=48 * 1024 * 1024
        ),
        name="eam",
    )(jitter, counts, inflow_jitter, inflow_counts, embed_weights)
    return pl.pallas_call(
        put_out,
        out_shape=tuple(jax.ShapeDtypeStruct(r.shape, f32) for r in raw),
        in_specs=[vmem] * 2,
        out_specs=(hbm, hbm),
        scratch_shapes=[dma((2,))],
        compiler_params=pltpu.CompilerParams(vmem_limit_bytes=1024 * 1024),
        name="put_out",
    )(*raw)


def put_out(forces, energy, forces_out, energy_out, sems):
    copies = [pltpu.make_async_copy(forces, forces_out, sems.at[0]),
              pltpu.make_async_copy(energy, energy_out, sems.at[1])]
    for copy in copies:
        copy.start()
    for copy in copies:
        copy.wait()


def solution(mesh):
    sizes = tuple(mesh.shape[a] for a in ("shock", "ty", "tz"))
    return jax.shard_map(
        functools.partial(on_device, sizes),
        mesh=mesh,
        in_specs=(
            P(None, None, "shock", "ty", "tz"),
            P("shock", "ty", "tz"),
            P(None, None, "ty", "tz"),
            P("ty", "tz"),
            P(),
        ),
        out_specs=(P(None, None, "shock", "ty", "tz"), P(None, "shock", "ty", "tz")),
        check_vma=False,
    )
```

profile of v0, /device:TPU:0, one launch (start us, length us, event | category | flops | bytes accessed | tf_op | source)
XLA Modules:
  0.0 31.5 jit_solution(10863024344056093540)
XLA Ops:
  0.6 0.0 copy-start
  0.6 0.9 %copy-done = f32[3,8,2,8,128]{4,3,2,1,0:T(8,128)S(1)} copy-done((f32[3,8,2,8,128]{4,3,2,1,0:T(8,128)S(1)}, f32[3,8,2,8,128]{4,3,2,1,0:T(8,128)}, u32[]{:S(2)}) %copy-start) | copy-done | bytes 196632
  1.6 0.0 copy-start.1
  1.6 0.9 %copy-done.1 = f32[3,8,8,128]{3,2,1,0:T(8,128)S(1)} copy-done((f32[3,8,8,128]{3,2,1,0:T(8,128)S(1)}, f32[3,8,8,128]{3,2,1,0:T(8,128)}, u32[]{:S(2)}) %copy-start.1) | copy-done | bytes 98328
  2.5 0.0 copy-start.2
  2.5 0.7 %copy-done.2 = s32[2,8,128]{2,1,0:T(8,128)S(1)} copy-done((s32[2,8,128]{2,1,0:T(8,128)S(1)}, s32[2,8,128]{2,1,0:T(8,128)}, u32[]{:S(2)}) %copy-start.2) | copy-done | bytes 8216
  3.1 0.0 copy-start.3
  3.2 0.7 %copy-done.3 = s32[8,128]{1,0:T(8,128)S(1)} copy-done((s32[8,128]{1,0:T(8,128)S(1)}, s32[8,128]{1,0:T(8,128)}, u32[]{:S(2)}) %copy-start.3) | copy-done | bytes 4120
  3.8 0.0 copy-start.4
  3.8 0.7 %copy-done.4 = f32[16]{0:T(128)S(1)} copy-done((f32[16]{0:T(128)S(1)}, f32[16]{0:T(128)}, u32[]{:S(2)}) %copy-start.4) | copy-done | bytes 88
  4.5 26.3 %eam.1 = (f32[3,8,2,8,128]{4,3,2,1,0:T(8,128)S(1)}, f32[8,2,8,128]{3,2,1,0:T(8,128)S(1)}) custom-call(f32[3,8,2,8,128]{4,3,2,1,0:T(8,128)S(1)} %copy-done, s32[2,8,128]{2,1,0:T(8,128)S(1)} %copy-done.2, f32[3,8,8,128]{3,2,1,0:T(8,128)S(1)} %copy-done.1, s32[8,128]{1,0:T(8,128)S(1)} %copy-done.3, f32[16]{0:T(128)S(1)} %copy-done.4), custom_call_target="tpu_custom_call" | custom-call | tf_op jit(solution)/shard_map/eam/pallas_call | solution.py:493
  30.8 0.7 %put_out.1 = (f32[3,8,2,8,128]{4,3,2,1,0:T(8,128)}, f32[8,2,8,128]{3,2,1,0:T(8,128)}) custom-call(f32[3,8,2,8,128]{4,3,2,1,0:T(8,128)S(1)} %get-tuple-element.4.forces, f32[8,2,8,128]{3,2,1,0:T(8,128)S(1)} %get-tuple-element.5.energy), custom_call_target="tpu_custom_call" | custom-call | tf_op jit(solution)/shard_map/put_out/pallas_call | solution.py:507
Async XLA Ops:
  0.6 0.9 %copy-start = (f32[3,8,2,8,128]{4,3,2,1,0:T(8,128)S(1)}, f32[3,8,2,8,128]{4,3,2,1,0:T(8,128)}, u32[]{:S(2)}) copy-start(f32[3,8,2,8,128]{4,3,2,1,0:T(8,128)} %jit_hbm.1) | copy-start | bytes 589828
  1.6 0.9 %copy-start.1 = (f32[3,8,8,128]{3,2,1,0:T(8,128)S(1)}, f32[3,8,8,128]{3,2,1,0:T(8,128)}, u32[]{:S(2)}) copy-start(f32[3,8,8,128]{3,2,1,0:T(8,128)} %ijit_hbm.1) | copy-start | bytes 294916
  2.5 0.7 %copy-start.2 = (s32[2,8,128]{2,1,0:T(8,128)S(1)}, s32[2,8,128]{2,1,0:T(8,128)}, u32[]{:S(2)}) copy-start(s32[2,8,128]{2,1,0:T(8,128)} %cnt_hbm.1) | copy-start | bytes 24580
  3.1 0.7 %copy-start.3 = (s32[8,128]{1,0:T(8,128)S(1)}, s32[8,128]{1,0:T(8,128)}, u32[]{:S(2)}) copy-start(s32[8,128]{1,0:T(8,128)} %icnt_hbm.1) | copy-start | bytes 12292
  3.8 0.7 %copy-start.4 = (f32[16]{0:T(128)S(1)}, f32[16]{0:T(128)}, u32[]{:S(2)}) copy-start(f32[16]{0:T(128)} %weights_hbm.1) | copy-start | bytes 196
where the time goes:
time: 31.7 us; the launch traced here: 31.5 us
  Pallas kernels  27 us (85%)
  local copies, waits for them, and re-layouts  3.85 us (12%)
  between operations  0.65 us (2%)
    pallas_call x1, Pallas kernels, on_device(): pl.pallas_call(functools.partial(kernel, sizes), out_shape=(jax.ShapeDtyp...  26.3 us
    unnamed x10, local copies, waits for them, and re-layouts  3.85 us
    pallas_call x1, Pallas kernels, on_device(): pl.pallas_call(put_out, out_shape=tuple((jax.ShapeDtypeStruct(r.shape, f3...  0.71 us

commit v1 on v0

--- a/solution.py
+++ b/solution.py
@@ -503,7 +503,7 @@
             collective_id=0, has_side_effects=True, vmem_limit_bytes=48 * 1024 * 1024
         ),
         name="eam",
-    )(jitter, counts, inflow_jitter, inflow_counts, embed_weights)
+    )(*(pltpu.with_memory_space_constraint(x, pltpu.HBM) for x in (jitter, counts, inflow_jitter, inflow_counts, embed_weights)))
     return pl.pallas_call(
         put_out,
         out_shape=tuple(jax.ShapeDtypeStruct(r.shape, f32) for r in raw),

time: 31.7 us -> 27.5 us (0.87)
  local copies, waits for them, and re-layouts: 3.85 us -> 0 us
  Pallas kernels: 27 us -> 26.6 us
    unnamed x10 -> x0, local copies, waits for them, and re-layouts: 3.85 us -> none
    pallas_call x1, Pallas kernels: 26.3 us -> 25.9 us  [on_device(): pl.pallas_call(functools.partial(kernel, sizes), out_shape=(jax.ShapeDtyp...]
where the time goes in v1:
time: 27.5 us; the launch traced here: 27.3 us
  Pallas kernels  26.6 us (97%)
  between operations  0.64 us (2%)
    pallas_call x1, Pallas kernels, on_device(): pl.pallas_call(functools.partial(kernel, sizes), out_shape=(jax.ShapeDtyp...  25.9 us
    pallas_call x1, Pallas kernels, on_device(): pl.pallas_call(put_out, out_shape=tuple((jax.ShapeDtypeStruct(r.shape, f3...  0.71 us

profile of v1, /device:TPU:0, one launch (start us, length us, event | category | flops | bytes accessed | tf_op | source)
XLA Modules:
  0.0 27.3 jit_solution(17570270148437809016)
XLA Ops:
  0.6 25.9 %eam.1 = (f32[3,8,2,8,128]{4,3,2,1,0:T(8,128)S(1)}, f32[8,2,8,128]{3,2,1,0:T(8,128)S(1)}) custom-call(f32[3,8,2,8,128]{4,3,2,1,0:T(8,128)} %jit_hbm.1, s32[2,8,128]{2,1,0:T(8,128)} %cnt_hbm.1, f32[3,8,8,128]{3,2,1,0:T(8,128)} %ijit_hbm.1, s32[8,128]{1,0:T(8,128)} %icnt_hbm.1, f32[16]{0:T(128)} %weights_hbm.1), custom_call_target="tpu_custom_call" | custom-call | tf_op jit(solution)/shard_map/eam/pallas_call | solution.py:493
  26.6 0.7 %put_out.1 = (f32[3,8,2,8,128]{4,3,2,1,0:T(8,128)}, f32[8,2,8,128]{3,2,1,0:T(8,128)}) custom-call(f32[3,8,2,8,128]{4,3,2,1,0:T(8,128)S(1)} %get-tuple-element.4.forces, f32[8,2,8,128]{3,2,1,0:T(8,128)S(1)} %get-tuple-element.5.energy), custom_call_target="tpu_custom_call" | custom-call | tf_op jit(solution)/shard_map/put_out/pallas_call | solution.py:507

commit v2 on v1

--- a/solution.py
+++ b/solution.py
@@ -8,18 +8,14 @@
 from jax.sharding import PartitionSpec as P
 
 MESH = pl.DeviceIdType.MESH
-FAR = 8.0
-ALL = [
-    (x, y, z)
-    for x in range(-2, 3)
-    for y in range(-2, 3)
-    for z in range(-2, 3)
-    if (x, y, z) != (0, 0, 0) and (abs(x) == 2) + (abs(y) == 2) + (abs(z) == 2) <= 1
-]
-PARTS = [[o for o in ALL if (o[1] in (0, 1), o[2] in (0, 1)) == inside]
+FAR = 40.0
+SIDES = [(y, z) for y in range(-2, 3) for z in range(-2, 3) if abs(y) + abs(z) < 4]
+COLUMNS = [((y, z), [x for x in range(-2, 3)
+                     if (x, y, z) != (0, 0, 0) and (abs(x) == 2) + (abs(y) == 2) + (abs(z) == 2) <= 1])
+           for y, z in SIDES]
+PARTS = [[o for o in COLUMNS if (o[0][0] in (0, 1), o[0][1] in (0, 1)) == inside]
          for inside in ((True, True), (False, True), (True, False), (False, False))]
-OFFSETS = sum(PARTS, [])
-STARTS = [sum(len(p) for p in PARTS[:k]) for k in range(len(PARTS))]
+OFFSETS = [(x, y, z) for part in PARTS for (y, z), steps in part for x in steps]
 DIRS = [(b, c) for b in (-1, 0, 1) for c in (-1, 0, 1) if (b, c) != (0, 0)]
 ROW_DIRS = (1, 6)
 COL_DIRS = (3, 4)
@@ -27,7 +23,12 @@
 ORDER = CORNER_DIRS + COL_DIRS + ROW_DIRS
 SLOTS = 8
 RIM = 2
-LOG2E = 1.4426950408889634
+KAPPA = 3.0 * 1.4426950408889634
+E0 = 0.22313016014842982
+DENSITY_SCALE = 16.0 / 6.0 * E0 / KAPPA**4
+PAIR_SCALE = 0.5 * 3.2 * E0 / KAPPA**4
+FORCE_SCALE = -19.2 * E0 * E0 / KAPPA**4
+SLOPE_SCALE = 1.0 / (2.4 * E0)
 
 
 def side(step):
@@ -36,7 +37,7 @@
 
 def kernel(sizes, jit_hbm, cnt_hbm, ijit_hbm, icnt_hbm, weights_hbm, forces, energy,
            jit, cnt, ijit, icnt, weights, dens, load, atoms, rows_out, cols_out, corn_out, rows_in, cols_in, corn_in,
-           site, terms, slope, emb, slope_site,
+           site, terms, slope, partial, slope_site,
            srow_out, scol_out, srow_in, scol_in, scor_in, slayer_in,
            send1, recv1, send_layer, recv_layer, send2, recv2, send_s, recv_s):
     n_shock, n_ty, n_tz = sizes
@@ -86,7 +87,7 @@
             count = jnp.where(leading, 0, count)
         for s in range(SLOTS):
             for c in range(3):
-                value = jit[c, s, l] + (0.25 + 0.5 * (s // 2**c % 2))
+                value = jit[c, s, l] * KAPPA + KAPPA * (0.25 + 0.5 * (s // 2**c % 2))
                 if c == 0:
                     value = jnp.where(s < count, value, value + FAR)
                 atoms[atom_rows(l, c, s), :] = value
@@ -128,8 +129,8 @@
         count = icnt[...]
         for s in range(SLOTS):
             for c in range(3):
-                base = 0.25 + 0.5 * (s // 2**c % 2)
-                value = ijit[c, s] + base
+                base = KAPPA * (0.25 + 0.5 * (s // 2**c % 2))
+                value = ijit[c, s] * KAPPA + base
                 if c == 0:
                     value = jnp.where(s < count, value, value + FAR)
                 atoms[atom_rows(layers, c, s), :] = value
@@ -198,10 +199,10 @@
         return c, 2 * e + bx, 2 * (b + 1) + by, 2 * (z + 1) + bz
 
     def moved(value, c, b, z):
-        return value + float(b) if c == 1 and b else (value + float(z) if c == 2 and z else value)
+        return value + KAPPA * b if c == 1 and b else (value + KAPPA * z if c == 2 and z else value)
 
     def build_centre(e, carry):
-        x_base = e.astype(jnp.float32)
+        x_base = e.astype(jnp.float32) * KAPPA
         for c in range(3):
             for s in range(SLOTS):
                 value = atoms[pl.ds(pl.multiple_of(((e * 3 + c) * SLOTS + s) * ny, ny), ny), :]
@@ -210,7 +211,7 @@
 
     def halo_rows(e, c, b):
         halo = rows_in[e // RIM, side(b), e % RIM, c]
-        return halo + e.astype(jnp.float32) if c == 0 else halo
+        return halo + e.astype(jnp.float32) * KAPPA if c == 0 else halo
 
     def build_y(e, carry):
         for c in range(3):
@@ -224,7 +225,7 @@
     def build_z(e, carry):
         for z in (-1, 1):
             columns = cols_in[e // RIM, side(z), e % RIM]
-            first = columns + e.astype(jnp.float32)
+            first = columns + e.astype(jnp.float32) * KAPPA
             for c in range(3):
                 for s in range(SLOTS):
                     out = with_edge_z(site[sites_of(e, c, s, 0, 0)], columns if c else first, c * SLOTS + s, z)
@@ -238,69 +239,78 @@
                 for z in (-1, 1):
                     corner = corn_in[e // RIM, side(b), side(z), e % RIM]
                     if c == 0:
-                        corner = corner + e.astype(jnp.float32)
+                        corner = corner + e.astype(jnp.float32) * KAPPA
                     halo_z = moved(with_edge_z(halo, corner, c, z), c, 0, z)
                     for s in range(SLOTS):
                         out = with_edge_y(site[sites_of(e, c, s, 0, z)], halo_z, s, b)
-                        site[sites_of(e, c, s, b, z)] = out + float(b) if c == 1 else out
+                        site[sites_of(e, c, s, b, z)] = out + KAPPA * b if c == 1 else out
         return carry
 
+    halves = 2 * layers
+
     def split(q):
-        return 2 + q // 4, 2 + q // 2 % 2, 2 + q % 2
-
-    def place_of(q):
-        x, y, z = split(q)
-        return x // 2 - 1, x % 2 + 2 * (y - 2) + 4 * (z - 2)
-
-    def near(q, offset):
-        x, y, z = split(q)
-        return (x + offset[0], y + offset[1] * (5 - 2 * y), z + offset[2] * (5 - 2 * z))
-
-    atoms_count = 2 * layers * 4
+        return q // 2, q % 2
+
+    def rows_of(k, q):
+        return pl.ds(pl.multiple_of((k // 2 * SLOTS + k % 2 + 2 * q) * ny, ny), ny)
+
+    def near(q, dy, dz):
+        z, y = split(q)
+        return 2 + y + dy * (1 - 2 * y), 2 + z + dz * (1 - 2 * z)
 
     def density_part(part, q, carry):
-        at = split(q)
-        px, py, pz = (site[(c,) + at] for c in range(3))
+        z, y = split(q)
+        centre = [[site[c, 2 + k, 2 + y, 2 + z] for c in range(3)] for k in range(halves)]
         zero = jnp.zeros((ny, nz), jnp.float32)
-        total = [dens[q] if part else zero, zero]
-        for k, offset in enumerate(PARTS[part]):
-            n = STARTS[part] + k
-            to = near(q, offset)
-            dx = site[(0,) + to] - px
-            dy = site[(1,) + to] - py
-            dz = site[(2,) + to] - pz
-            squared = dx * dx + dy * dy + dz * dz
-            inverse = lax.rsqrt(squared)
-            radius = squared * inverse
-            inside = jnp.maximum(1.0 - radius, 0.0)
-            decay = jnp.exp(1.5 - 3.0 * radius)
-            inside2 = inside * inside
-            total[k % 2] = total[k % 2] + decay * (inside2 * inside2)
-            terms[0, q, n] = inside
-            terms[1, q, n] = decay
-            terms[2, q, n] = inverse
+        total = [dens[0, q, k] if part else zero for k in range(halves)]
+        power = [dens[1, q, k] if part else zero for k in range(halves)]
+        for (dy, dz), steps in PARTS[part]:
+            to = near(q, dy, dz)
+            for x in range(2 + min(steps), 2 + halves + max(steps)):
+                inner = [k for k in range(halves) if x - 2 - k in steps]
+                if not inner:
+                    continue
+                other = [site[(c, x) + to] for c in range(3)]
+                for k in inner:
+                    n = OFFSETS.index((x - 2 - k, dy, dz))
+                    dx, dy_, dz_ = (other[c] - centre[k][c] for c in range(3))
+                    squared = dx * dx + dy_ * dy_ + dz_ * dz_
+                    inverse = lax.rsqrt(squared)
+                    inside = jnp.maximum(KAPPA - squared * inverse, 0.0)
+                    decay = jnp.exp2(inside)
+                    cube = inside * inside * inside * decay
+                    value = cube * inside
+                    total[k] = total[k] + value
+                    power[k] = power[k] + decay * value
+                    scaled = cube * inverse
+                    terms[0, q, k, n] = scaled * (inside + 4.0 / 3.0 * KAPPA)
+                    terms[1, q, k, n] = scaled * (decay * (inside + 2.0 / 3.0 * KAPPA))
         if part < len(PARTS) - 1:
-            dens[q] = total[0] + total[1]
+            for k in range(halves):
+                dens[0, q, k] = total[k]
+                dens[1, q, k] = power[k]
             return carry
-        l, s = place_of(q)
-        density = (total[0] + total[1]) * (16.0 / 6.0)
-        root = jnp.sqrt(1.0 + density)
-        value = -root
-        grad = -0.5 / root
-        for k in range(weights.shape[0]):
-            scaled = density * 4.0 - float(k)
-            bump = weights[k] * jnp.exp(-0.5 * scaled * scaled)
-            value = value + bump
-            grad = grad - bump * scaled * 4.0
-        emb[q] = value
-        slope[pl.ds(pl.multiple_of((l * SLOTS + s) * ny, ny), ny), :] = grad
+        for k in range(halves):
+            density = total[k] * DENSITY_SCALE
+            root = jnp.sqrt(1.0 + density)
+            value = -root
+            grad = -0.5 / root
+            for w in range(weights.shape[0]):
+                scaled = density * 4.0 - float(w)
+                bump = weights[w] * jnp.exp(-0.5 * scaled * scaled)
+                value = value + bump
+                grad = grad - bump * scaled * 4.0
+            value = value + (E0 * power[k] - 2.0 * total[k]) * PAIR_SCALE
+            occupied = centre[k][0] - (1 + k // 2) * KAPPA < 0.5 * FAR
+            energy[2 * q + k % 2, k // 2] = jnp.where(occupied, value, 0.0)
+            slope[rows_of(k, q), :] = (grad - 1.2) * SLOPE_SCALE
         return carry
 
     for part, (dirs, build) in enumerate((
             ((), build_centre), (ROW_DIRS, build_y), (COL_DIRS, build_z), (CORNER_DIRS, build_corners))):
         arrived(dirs)
         lax.fori_loop(0, ext, build, 0)
-        lax.fori_loop(0, atoms_count, functools.partial(density_part, part), 0)
+        lax.fori_loop(0, 4, functools.partial(density_part, part), 0)
 
     for l in range(layers):
         for yi, edge in ((0, 0), (1, ny - 1)):
@@ -342,21 +352,6 @@
                 copy2(a, d).start()
         guarded(a, run)
 
-    def pair_step(q, carry):
-        pair = [jnp.zeros((ny, nz), jnp.float32) for _ in range(2)]
-        for n in range(len(OFFSETS)):
-            inside, decay, inverse = (terms[i, q, n] for i in range(3))
-            cube = inside * inside * inside * decay
-            lower = decay - 2.0
-            pair[n % 2] = pair[n % 2] + cube * inside * lower
-            scaled = cube * inverse
-            terms[0, q, n] = scaled * (-8.0 * inside - 32.0 / 3.0)
-            terms[1, q, n] = scaled * (-19.2 * inside * (decay - 1.0) - 12.8 * lower)
-        emb[q] = emb[q] + (0.5 * 3.2) * (pair[0] + pair[1])
-        return carry
-
-    lax.fori_loop(0, atoms_count, pair_step, 0)
-
     for a in (-1, 1):
         @pl.when(jnp.logical_not(exists(a)))
         def _(a=a):
@@ -378,27 +373,35 @@
             guarded(a, run)
 
     def force_part(part, q, carry):
-        x, y, z = split(q)
-        l, s = place_of(q)
-        at = (x, y, z)
-        centre = [site[(c,) + at] for c in range(3)]
-        own = slope_site[at]
+        z, y = split(q)
+        own = [slope_site[2 + k, 2 + y, 2 + z] for k in range(halves)]
         zero = jnp.zeros((ny, nz), jnp.float32)
-        total = [[forces[c, s, l] if part else zero, zero] for c in range(3)]
-        for k, offset in enumerate(PARTS[part]):
-            n = STARTS[part] + k
-            to = near(q, offset)
-            weight = (own + slope_site[to]) * terms[0, q, n] + terms[1, q, n]
+        total = [[partial[c, q, k] if part else zero for c in range(4)] for k in range(halves)]
+        for (dy, dz), steps in PARTS[part]:
+            to = near(q, dy, dz)
+            for x in range(2 + min(steps), 2 + halves + max(steps)):
+                inner = [k for k in range(halves) if x - 2 - k in steps]
+                if not inner:
+                    continue
+                other = [site[(c, x) + to] for c in range(3)]
+                theirs = slope_site[(x,) + to]
+                for k in inner:
+                    n = OFFSETS.index((x - 2 - k, dy, dz))
+                    weight = (own[k] + theirs) * terms[0, q, k, n] + terms[1, q, k, n]
+                    for c in range(3):
+                        total[k][c] = total[k][c] + weight * other[c]
+                    total[k][3] = total[k][3] + weight
+        if part < len(PARTS) - 1:
+            for k in range(halves):
+                for c in range(4):
+                    partial[c, q, k] = total[k][c]
+            return carry
+        for k in range(halves):
+            centre = [site[c, 2 + k, 2 + y, 2 + z] for c in range(3)]
+            occupied = centre[0] - (1 + k // 2) * KAPPA < 0.5 * FAR
             for c in range(3):
-                total[c][k % 2] = total[c][k % 2] + weight * (site[(c,) + to] - centre[c])
-        if part < len(PARTS) - 1:
-            for c in range(3):
-                forces[c, s, l] = total[c][0] + total[c][1]
-            return carry
-        occupied = centre[0] - (x // 2).astype(jnp.float32) < 0.5 * FAR
-        for c in range(3):
-            forces[c, s, l] = jnp.where(occupied, total[c][0] + total[c][1], 0.0)
-        energy[s, l] = jnp.where(occupied, emb[q], 0.0)
+                value = (total[k][c] - total[k][3] * centre[c]) * FORCE_SCALE
+                forces[c, 2 * q + k % 2, k // 2] = jnp.where(occupied, value, 0.0)
         return carry
 
     for part, dirs in enumerate(((), ROW_DIRS, COL_DIRS, CORNER_DIRS)):
@@ -432,7 +435,7 @@
                         for s in range(SLOTS):
                             slope_site[slope_at(e, s, b, z)] = with_edge_y(
                                 slope_site[slope_at(e, s, 0, z)], halo, s, b)
-        lax.fori_loop(0, atoms_count, functools.partial(force_part, part), 0)
+        lax.fori_loop(0, 4, functools.partial(force_part, part), 0)
 
     pl.when(me > 0)(lambda: layer_copy().wait_send())
     for_groups(lambda copy: copy.wait_send())
@@ -461,7 +464,7 @@
         pltpu.VMEM(inflow_jitter.shape, f32),
         pltpu.VMEM(inflow_counts.shape, counts.dtype),
         pltpu.SMEM(embed_weights.shape, f32),
-        pltpu.VMEM((layers * slots,) + tile, f32),
+        pltpu.VMEM((2, 4, 2 * layers) + tile, f32),
         dma((5,)),
         pltpu.VMEM((ext * dims * slots * ny, nz), f32),
         pltpu.VMEM((2, 2, RIM, dims) + (slots, nz), f32),
@@ -471,9 +474,9 @@
         pltpu.VMEM((2, 2, RIM) + tile, f32),
         pltpu.VMEM((2, 2, 2, RIM) + (slots, nz), f32),
         pltpu.VMEM((dims, 2 * ext, 6, 6) + tile, f32),
-        pltpu.VMEM((3, layers * slots, n) + tile, f32),
+        pltpu.VMEM((2, 4, 2 * layers, n) + tile, f32),
         pltpu.VMEM((layers * slots * ny, nz), f32),
-        pltpu.VMEM((layers * slots,) + tile, f32),
+        pltpu.VMEM((4, 4, 2 * layers) + tile, f32),
         pltpu.VMEM((2 * ext, 6, 6) + tile, f32),
         pltpu.VMEM((2, layers) + (slots, nz), f32),
         pltpu.VMEM((2, layers) + tile, f32),

time: 27.5 us -> 26.1 us (0.949)
  Pallas kernels: 26.6 us -> 25.2 us
    pallas_call x1, Pallas kernels: 25.9 us -> 24.5 us  [on_device(): pl.pallas_call(functools.partial(kernel, sizes), out_shape=(jax.ShapeDtyp...]
where the time goes in v2:
time: 26.1 us; the launch traced here: 25.8 us
  Pallas kernels  25.2 us (97%)
  between operations  0.64 us (2%)
    pallas_call x1, Pallas kernels, on_device(): pl.pallas_call(functools.partial(kernel, sizes), out_shape=(jax.ShapeDtyp...  24.5 us
    pallas_call x1, Pallas kernels, on_device(): pl.pallas_call(put_out, out_shape=tuple((jax.ShapeDtypeStruct(r.shape, f3...  0.71 us

profile of v2, /device:TPU:0, one launch (start us, length us, event | category | flops | bytes accessed | tf_op | source)
XLA Modules:
  0.0 25.8 jit_solution(7820947795472775909)
XLA Ops:
  0.6 24.5 %eam.1 = (f32[3,8,2,8,128]{4,3,2,1,0:T(8,128)S(1)}, f32[8,2,8,128]{3,2,1,0:T(8,128)S(1)}) custom-call(f32[3,8,2,8,128]{4,3,2,1,0:T(8,128)} %jit_hbm.1, s32[2,8,128]{2,1,0:T(8,128)} %cnt_hbm.1, f32[3,8,8,128]{3,2,1,0:T(8,128)} %ijit_hbm.1, s32[8,128]{1,0:T(8,128)} %icnt_hbm.1, f32[16]{0:T(128)} %weights_hbm.1), custom_call_target="tpu_custom_call" | custom-call | tf_op jit(solution)/shard_map/eam/pallas_call | solution.py:496
  25.1 0.7 %put_out.1 = (f32[3,8,2,8,128]{4,3,2,1,0:T(8,128)}, f32[8,2,8,128]{3,2,1,0:T(8,128)}) custom-call(f32[3,8,2,8,128]{4,3,2,1,0:T(8,128)S(1)} %get-tuple-element.4.forces, f32[8,2,8,128]{3,2,1,0:T(8,128)S(1)} %get-tuple-element.5.energy), custom_call_target="tpu_custom_call" | custom-call | tf_op jit(solution)/shard_map/put_out/pallas_call | solution.py:510

commit v3 on v2

--- a/solution.py
+++ b/solution.py
@@ -37,8 +37,8 @@
 
 def kernel(sizes, jit_hbm, cnt_hbm, ijit_hbm, icnt_hbm, weights_hbm, forces, energy,
            jit, cnt, ijit, icnt, weights, dens, load, atoms, rows_out, cols_out, corn_out, rows_in, cols_in, corn_in,
-           site, terms, slope, partial, slope_site,
-           srow_out, scol_out, srow_in, scol_in, scor_in, slayer_in,
+           site, terms, slope, emb, partial, slope_site,
+           srow_out, scol_out, scor_out, srow_in, scol_in, scor_in, slayer_in,
            send1, recv1, send_layer, recv_layer, send2, recv2, send_s, recv_s):
     n_shock, n_ty, n_tz = sizes
     layers, ny, nz = cnt.shape
@@ -96,31 +96,31 @@
         shift = (target - source) % nz
         return value if shift == 0 else pltpu.roll(value, shift, 1)
 
+    def gathered(pieces, start):
+        packed = None
+        for k, (value, source) in enumerate(pieces):
+            moved = place(value, source, start + k)
+            packed = moved if packed is None else jnp.where(lane == start + k, moved, packed)
+        return packed
+
     def pack(g, base):
-        for l in range(RIM):
-            for yi, edge in ((0, 0), (1, ny - 1)):
-                found = []
+        for yi, edge in ((0, 0), (1, ny - 1)):
+            found = []
+            for l in range(RIM):
                 for c in range(3):
                     start = ((base + l) * 3 + c) * SLOTS * ny + edge
                     value = atoms[pl.ds(start, SLOTS, stride=ny), :]
                     rows_out[g, yi, l, c] = value
                     found.append(value)
-                for zi, zedge in ((0, 0), (1, nz - 1)):
-                    packed = place(found[0], zedge, 0)
-                    for c in (1, 2):
-                        packed = jnp.where(lane == c, place(found[c], zedge, c), packed)
-                    corn_out[g, yi, zi, l] = packed
             for zi, zedge in ((0, 0), (1, nz - 1)):
-                parts = []
-                for c in range(3):
-                    packed = None
-                    for s in range(SLOTS):
-                        k = c * SLOTS + s
-                        moved = place(atoms[atom_rows(base + l, c, s), :], zedge, k)
-                        packed = moved if packed is None else jnp.where(lane == k, moved, packed)
-                    parts.append(packed)
-                packed = jnp.where(lane < SLOTS, parts[0], jnp.where(lane < 2 * SLOTS, parts[1], parts[2]))
-                cols_out[g, zi, l] = packed
+                corn_out[g, yi, zi] = gathered([(value, zedge) for value in found], 0)
+        for zi, zedge in ((0, 0), (1, nz - 1)):
+            packed = None
+            for k in range(RIM * 3):
+                tiles = [(atoms[atom_rows(base + k // 3, k % 3, s), :], zedge) for s in range(SLOTS)]
+                part = gathered(tiles, k * SLOTS)
+                packed = part if packed is None else jnp.where(lane < k * SLOTS, packed, part)
+            cols_out[g, zi] = packed
 
     pack(0, 0)
 
@@ -137,6 +137,16 @@
                 atoms[atom_rows(layers + 1, c, s), :] = jnp.full((ny, nz), base + (FAR if c == 0 else 0.0), jnp.float32)
         pack(1, layers)
 
+    def empty_rows(h, l):
+        slot = lax.broadcasted_iota(jnp.int32, (SLOTS, nz), 0)
+        for b in (-1, 1):
+            for c in range(3):
+                site_c = KAPPA * (0.25 + 0.5 * (slot // 2**c % 2).astype(jnp.float32))
+                rows_in[h, side(b), l, c] = site_c + FAR if c == 0 else site_c
+
+    pl.when(leading)(lambda: empty_rows(0, 0))
+    pl.when(trailing)(lambda: empty_rows(1, 1))
+
     ends = jnp.where(leading, 1, 0) + jnp.where(trailing, 1, 0)
     pl.semaphore_wait(barrier, 26 - 9 * ends)
 
@@ -149,41 +159,51 @@
             send_sem=send_layer, recv_sem=recv_layer,
             device_id=device(-1, 0, 0), device_id_type=MESH)
 
-    def ends1(g, h, b, c):
+    def ends1(g, h, b, c, kept):
         if c == 0:
-            return rows_out.at[g, side(b)], rows_in.at[h, side(-b)]
+            return rows_out.at[g, side(b), kept], rows_in.at[h, side(-b), kept]
         if b == 0:
             return cols_out.at[g, side(c)], cols_in.at[h, side(-c)]
         return corn_out.at[g, side(b), side(c)], corn_in.at[h, side(-b), side(-c)]
 
-    def copy1(group, g, h, a, d):
+    def copy1(group, g, h, a, d, kept):
         b, c = DIRS[d]
-        src, dst = ends1(g, h, b, c)
+        src, dst = ends1(g, h, b, c, kept)
         return pltpu.make_async_remote_copy(
             src_ref=src, dst_ref=dst, send_sem=send1.at[group, d],
             recv_sem=recv1.at[h, len(DIRS) - 1 - d],
             device_id=device(a, b, c), device_id_type=MESH)
 
-    groups = ((0, 0, 0, 0, None), (1, 0, 1, -1, me > 0), (2, 1, 1, 0, trailing))
+    everything, first, last = pl.ds(0, RIM), pl.ds(0, 1), pl.ds(1, 1)
 
     def for_groups(fn):
-        for group, g, h, a, cond in groups:
-            def run(group=group, g=g, h=h, a=a):
-                for d in ORDER:
-                    fn(copy1(group, g, h, a, d))
-            if cond is None:
-                run()
-            else:
-                pl.when(cond)(run)
+        def run(group, g, h, a, kept, dirs):
+            for d in dirs:
+                fn(copy1(group, g, h, a, d, kept))
+
+        run(0, 0, 0, 0, everything, CORNER_DIRS + COL_DIRS)
+        pl.when(leading)(lambda: run(0, 0, 0, 0, last, ROW_DIRS))
+        pl.when(me > 0)(lambda: run(0, 0, 0, 0, everything, ROW_DIRS))
+        pl.when(me > 0)(lambda: run(1, 0, 1, -1, everything, ORDER))
+        pl.when(trailing)(lambda: run(2, 1, 1, 0, first, ORDER))
 
     pl.when(me > 0)(lambda: layer_copy().start())
     for_groups(lambda copy: copy.start())
 
     pl.when(me < n_shock - 1)(lambda: layer_copy().wait_recv())
     def arrived(dirs):
-        for h in range(2):
+        def wait(h, kept):
             for d in dirs:
-                copy1(0, 0, h, 0, d).wait_recv()
+                copy1(0, 0, h, 0, d, kept).wait_recv()
+
+        if dirs == ROW_DIRS:
+            pl.when(leading)(lambda: wait(0, last))
+            pl.when(me > 0)(lambda: wait(0, everything))
+            pl.when(trailing)(lambda: wait(1, first))
+            pl.when(me < n_shock - 1)(lambda: wait(1, everything))
+        else:
+            wait(0, everything)
+            wait(1, everything)
 
     def with_edge_z(value, column, source, step):
         edge = nz - 1 if step > 0 else 0
@@ -224,7 +244,7 @@
 
     def build_z(e, carry):
         for z in (-1, 1):
-            columns = cols_in[e // RIM, side(z), e % RIM]
+            columns = pltpu.roll(cols_in[e // RIM, side(z)], lax.rem(nz - e % RIM * (3 * SLOTS), nz), 1)
             first = columns + e.astype(jnp.float32) * KAPPA
             for c in range(3):
                 for s in range(SLOTS):
@@ -237,7 +257,7 @@
             for b in (-1, 1):
                 halo = halo_rows(e, c, b)
                 for z in (-1, 1):
-                    corner = corn_in[e // RIM, side(b), side(z), e % RIM]
+                    corner = pltpu.roll(corn_in[e // RIM, side(b), side(z)], lax.rem(nz - e % RIM * 3, nz), 1)
                     if c == 0:
                         corner = corner + e.astype(jnp.float32) * KAPPA
                     halo_z = moved(with_edge_z(halo, corner, c, z), c, 0, z)
@@ -262,8 +282,7 @@
         z, y = split(q)
         centre = [[site[c, 2 + k, 2 + y, 2 + z] for c in range(3)] for k in range(halves)]
         zero = jnp.zeros((ny, nz), jnp.float32)
-        total = [dens[0, q, k] if part else zero for k in range(halves)]
-        power = [dens[1, q, k] if part else zero for k in range(halves)]
+        total = [dens[q, k] if part else zero for k in range(halves)]
         for (dy, dz), steps in PARTS[part]:
             to = near(q, dy, dz)
             for x in range(2 + min(steps), 2 + halves + max(steps)):
@@ -278,17 +297,14 @@
                     inverse = lax.rsqrt(squared)
                     inside = jnp.maximum(KAPPA - squared * inverse, 0.0)
                     decay = jnp.exp2(inside)
-                    cube = inside * inside * inside * decay
-                    value = cube * inside
-                    total[k] = total[k] + value
-                    power[k] = power[k] + decay * value
-                    scaled = cube * inverse
-                    terms[0, q, k, n] = scaled * (inside + 4.0 / 3.0 * KAPPA)
-                    terms[1, q, k, n] = scaled * (decay * (inside + 2.0 / 3.0 * KAPPA))
+                    square = inside * inside
+                    total[k] = total[k] + decay * (square * square)
+                    terms[0, q, k, n] = inside
+                    terms[1, q, k, n] = decay
+                    terms[2, q, k, n] = inverse
         if part < len(PARTS) - 1:
             for k in range(halves):
-                dens[0, q, k] = total[k]
-                dens[1, q, k] = power[k]
+                dens[q, k] = total[k]
             return carry
         for k in range(halves):
             density = total[k] * DENSITY_SCALE
@@ -300,9 +316,7 @@
                 bump = weights[w] * jnp.exp(-0.5 * scaled * scaled)
                 value = value + bump
                 grad = grad - bump * scaled * 4.0
-            value = value + (E0 * power[k] - 2.0 * total[k]) * PAIR_SCALE
-            occupied = centre[k][0] - (1 + k // 2) * KAPPA < 0.5 * FAR
-            energy[2 * q + k % 2, k // 2] = jnp.where(occupied, value, 0.0)
+            emb[q, k] = value - 2.0 * PAIR_SCALE * total[k]
             slope[rows_of(k, q), :] = (grad - 1.2) * SLOPE_SCALE
         return carry
 
@@ -312,22 +326,22 @@
         lax.fori_loop(0, ext, build, 0)
         lax.fori_loop(0, 4, functools.partial(density_part, part), 0)
 
-    for l in range(layers):
-        for yi, edge in ((0, 0), (1, ny - 1)):
-            srow_out[yi, l] = slope[pl.ds(l * SLOTS * ny + edge, SLOTS, stride=ny), :]
+    for yi, edge in ((0, 0), (1, ny - 1)):
+        found = [slope[pl.ds(l * SLOTS * ny + edge, SLOTS, stride=ny), :] for l in range(layers)]
+        for l in range(layers):
+            srow_out[yi, l] = found[l]
         for zi, zedge in ((0, 0), (1, nz - 1)):
-            packed = None
-            for s in range(SLOTS):
-                moved = place(slope[pl.ds((l * SLOTS + s) * ny, ny), :], zedge, s)
-                packed = moved if packed is None else jnp.where(lane == s, moved, packed)
-            scol_out[zi, l] = packed
+            scor_out[yi, zi] = gathered([(value, zedge) for value in found], 0)
+    for zi, zedge in ((0, 0), (1, nz - 1)):
+        scol_out[zi] = gathered([(slope[pl.ds(k * ny, ny), :], zedge) for k in range(layers * SLOTS)], 0)
 
     def ends2(a, b, c):
+        kept = pl.ds(0, layers) if a == 0 else pl.ds(0 if a < 0 else layers - 1, 1)
         if c == 0:
-            return srow_out.at[side(b)], srow_in.at[1 - a, side(-b)]
+            return srow_out.at[side(b), kept], srow_in.at[1 - a, side(-b), kept]
         if b == 0:
             return scol_out.at[side(c)], scol_in.at[1 - a, side(-c)]
-        return srow_out.at[side(b)], scor_in.at[1 - a, side(-b), side(-c)]
+        return scor_out.at[side(b), side(c)], scor_in.at[1 - a, side(-b), side(-c)]
 
     def copy2(a, d):
         b, c = DIRS[d]
@@ -351,6 +365,25 @@
             for d in ORDER:
                 copy2(a, d).start()
         guarded(a, run)
+
+    def pair_step(t, carry):
+        q, k = t // halves, lax.rem(t, halves)
+        power = [jnp.zeros((ny, nz), jnp.float32) for _ in range(2)]
+        for n in range(len(OFFSETS)):
+            inside, decay, inverse = (terms[i, q, k, n] for i in range(3))
+            cube = inside * inside * inside * decay
+            power[n % 2] = power[n % 2] + decay * (cube * inside)
+            scaled = cube * inverse
+            terms[0, q, k, n] = scaled * (inside + 4.0 / 3.0 * KAPPA)
+            terms[1, q, k, n] = scaled * (decay * (inside + 2.0 / 3.0 * KAPPA))
+        value = emb[q, k] + (E0 * PAIR_SCALE) * (power[0] + power[1])
+        z, y = split(q)
+        x_cell = (1 + k // 2).astype(jnp.float32) * KAPPA
+        occupied = site[0, 2 + k, 2 + y, 2 + z] - x_cell < 0.5 * FAR
+        energy[2 * q + lax.rem(k, 2), k // 2] = jnp.where(occupied, value, 0.0)
+        return carry
+
+    lax.fori_loop(0, 4 * halves, pair_step, 0)
 
     for a in (-1, 1):
         @pl.when(jnp.logical_not(exists(a)))
@@ -423,15 +456,14 @@
                             slope_site[slope_at(e, s, 0, 0)], halo, s, b)
             elif part == 2:
                 for z in steps:
-                    columns = scol_in[a, side(z), l]
+                    columns = scol_in[a, side(z)]
                     for s in range(SLOTS):
                         slope_site[slope_at(e, s, 0, z)] = with_edge_z(
-                            slope_site[slope_at(e, s, 0, 0)], columns, s, z)
+                            slope_site[slope_at(e, s, 0, 0)], columns, l * SLOTS + s, z)
             else:
                 for b in steps:
                     for z in steps:
-                        halo = with_edge_z(srow_in[a, side(b), l], scor_in[a, side(b), side(z), l],
-                                           0 if z > 0 else nz - 1, z)
+                        halo = with_edge_z(srow_in[a, side(b), l], scor_in[a, side(b), side(z)], l, z)
                         for s in range(SLOTS):
                             slope_site[slope_at(e, s, b, z)] = with_edge_y(
                                 slope_site[slope_at(e, s, 0, z)], halo, s, b)
@@ -464,25 +496,27 @@
         pltpu.VMEM(inflow_jitter.shape, f32),
         pltpu.VMEM(inflow_counts.shape, counts.dtype),
         pltpu.SMEM(embed_weights.shape, f32),
-        pltpu.VMEM((2, 4, 2 * layers) + tile, f32),
+        pltpu.VMEM((4, 2 * layers) + tile, f32),
         dma((5,)),
         pltpu.VMEM((ext * dims * slots * ny, nz), f32),
         pltpu.VMEM((2, 2, RIM, dims) + (slots, nz), f32),
-        pltpu.VMEM((2, 2, RIM) + tile, f32),
-        pltpu.VMEM((2, 2, 2, RIM) + (slots, nz), f32),
+        pltpu.VMEM((2, 2) + tile, f32),
+        pltpu.VMEM((2, 2, 2) + (slots, nz), f32),
         pltpu.VMEM((2, 2, RIM, dims) + (slots, nz), f32),
-        pltpu.VMEM((2, 2, RIM) + tile, f32),
-        pltpu.VMEM((2, 2, 2, RIM) + (slots, nz), f32),
+        pltpu.VMEM((2, 2) + tile, f32),
+        pltpu.VMEM((2, 2, 2) + (slots, nz), f32),
         pltpu.VMEM((dims, 2 * ext, 6, 6) + tile, f32),
-        pltpu.VMEM((2, 4, 2 * layers, n) + tile, f32),
+        pltpu.VMEM((3, 4, 2 * layers, n) + tile, f32),
         pltpu.VMEM((layers * slots * ny, nz), f32),
+        pltpu.VMEM((4, 2 * layers) + tile, f32),
         pltpu.VMEM((4, 4, 2 * layers) + tile, f32),
         pltpu.VMEM((2 * ext, 6, 6) + tile, f32),
         pltpu.VMEM((2, layers) + (slots, nz), f32),
-        pltpu.VMEM((2, layers) + tile, f32),
+        pltpu.VMEM((2,) + tile, f32),
+        pltpu.VMEM((2, 2) + (slots, nz), f32),
         pltpu.VMEM((3, 2, layers) + (slots, nz), f32),
-        pltpu.VMEM((3, 2, layers) + tile, f32),
-        pltpu.VMEM((3, 2, 2, layers) + (slots, nz), f32),
+        pltpu.VMEM((3, 2) + tile, f32),
+        pltpu.VMEM((3, 2, 2) + (slots, nz), f32),
         pltpu.VMEM((2, slots * ny, nz), f32),
         dma((3, len(DIRS))),
         dma((2, len(DIRS))),

time: 26.1 us -> 24.3 us (0.931)
  Pallas kernels: 25.2 us -> 23.4 us
    pallas_call x1, Pallas kernels: 24.5 us -> 22.7 us  [on_device(): pl.pallas_call(functools.partial(kernel, sizes), out_shape=(jax.ShapeDtyp...]
where the time goes in v3:
time: 24.3 us; the launch traced here: 24.1 us
  Pallas kernels  23.4 us (96%)
  between operations  0.64 us (3%)
    pallas_call x1, Pallas kernels, on_device(): pl.pallas_call(functools.partial(kernel, sizes), out_shape=(jax.ShapeDtyp...  22.7 us
    pallas_call x1, Pallas kernels, on_device(): pl.pallas_call(put_out, out_shape=tuple((jax.ShapeDtypeStruct(r.shape, f3...  0.71 us

profile of v3, /device:TPU:0, one launch (start us, length us, event | category | flops | bytes accessed | tf_op | source)
XLA Modules:
  0.0 24.1 jit_solution(16291078545913541884)
XLA Ops:
  0.6 22.7 %eam.1 = (f32[3,8,2,8,128]{4,3,2,1,0:T(8,128)S(1)}, f32[8,2,8,128]{3,2,1,0:T(8,128)S(1)}) custom-call(f32[3,8,2,8,128]{4,3,2,1,0:T(8,128)} %jit_hbm.1, s32[2,8,128]{2,1,0:T(8,128)} %cnt_hbm.1, f32[3,8,8,128]{3,2,1,0:T(8,128)} %ijit_hbm.1, s32[8,128]{1,0:T(8,128)} %icnt_hbm.1, f32[16]{0:T(128)} %weights_hbm.1), custom_call_target="tpu_custom_call" | custom-call | tf_op jit(solution)/shard_map/eam/pallas_call | solution.py:530
  23.4 0.7 %put_out.1 = (f32[3,8,2,8,128]{4,3,2,1,0:T(8,128)}, f32[8,2,8,128]{3,2,1,0:T(8,128)}) custom-call(f32[3,8,2,8,128]{4,3,2,1,0:T(8,128)S(1)} %get-tuple-element.4.forces, f32[8,2,8,128]{3,2,1,0:T(8,128)S(1)} %get-tuple-element.5.energy), custom_call_target="tpu_custom_call" | custom-call | tf_op jit(solution)/shard_map/put_out/pallas_call | solution.py:544
